TPU v7x, 1024 devices: a whole 4x8x16 slice. The times are simulated.
1024 devices in a mesh: zone: 16 (over y, core), grp: 64 (over z, x).
Axes of the slice: x: 4, y: 8, z: 16, core: 2. Of those that a mesh axis runs over, the one named last changes fastest.
Arguments:
- positions: float32 [3, 2097152], P(None, ('zone', 'grp')), may hold values from 0 to 1
- masses: float32 [2097152], P(('zone', 'grp')), may hold values from 0.0009765625 to 0.015625
- active: int32 [2097152], P(('zone', 'grp')), may hold values 0 or 1
- near_src: int32 [8192, 8], P(('zone', 'grp')), may hold values from 0 to 511, as said below
- multipoles: bfloat16 [81, 32768], P(None, ('zone', 'grp')), may hold values from -6 to 6
- far_src: int32 [32768, 189], P(('zone', 'grp')), may hold values from 0 to 95
- far_class: int32 [32768, 189], P(('zone', 'grp')), may hold values from 0 to 315
- m2l_ops: bfloat16 [81, 25596], replicated, may hold values from -0.046875 to 0.046875
Outputs:
- accel: float32 [3, 2097152], P(None, ('zone', 'grp'))
- local_coeffs: float32 [81, 32768], P(None, ('zone', 'grp'))
Inputs may be any that keep to these rules, and one draw needn't show every extreme that they name: `near_src`: of the 64 entries of one device's rows, at most 2 name leaves held by any one device of the zone (leaves s * 8 to s * 8 + 7 for device s), and exactly 2 name those of some device.
All inputs are finite; a program needn't handle non-finite values. No bound on the sum of `active` on one device may be relied on, other than what follows from the above.
Results may differ from a plain program's by a relative error of at most 0.0021.
Values may be sent and summed in bfloat16 or wider, within the bound.
A program may use at most 32 MiB of HBM per device.

v0:
```python
import jax
import jax.numpy as jnp
from jax import lax
from jax.sharding import PartitionSpec as P

softening = 0.0025


def side_by_side(arrays, axis, split_dim, concat_dim, along):
    columns = [a.reshape(*a.shape[:along], -1) for a in arrays]
    both = jnp.concatenate(columns, axis=along)
    filled, at, outs = (
        lax.all_to_all(both, axis, split_axis=split_dim, concat_axis=concat_dim, tiled=True),
        0,
        [],
    )
    for a, column in zip(arrays, columns):
        section = filled[..., at : at + column.shape[along]]
        outs.append(section.reshape(*section.shape[:along], *a.shape[along:]))
        at += column.shape[along]
    return tuple(outs)


def with_halo(value, sides, width):
    for axis, dim in sides:
        devices, length = (lax.axis_size(axis), value.shape[dim])
        up = [(i, (i + 1) % devices) for i in range(devices - 1)]
        down = [(j, i) for i, j in up]
        last = lax.slice_in_dim(value, length - width, length, axis=dim)
        leading = lax.slice_in_dim(value, 0, width, axis=dim)
        before = lax.ppermute(last, axis, up)
        after = lax.ppermute(leading, axis, down)
        value = jnp.concatenate([before, value, after], axis=dim)
    return value


def one_pair(operands):
    tpos, spos, smass = operands
    delta = spos[:, None, :] - tpos[:, :, None]
    dist2 = jnp.sum(delta * delta, axis=0) + softening
    weight = smass[None, :] * lax.rsqrt(dist2) / dist2
    return jnp.sum(delta * weight[None], axis=2)


def item_forces(tpos, spos, smass):
    return lax.map(one_pair, (tpos, spos, smass), batch_size=8)


def on_device(positions, masses, active, near_src, multipoles, far_src, far_class, m2l_ops):
    leaves, near = near_src.shape
    width = positions.shape[1] // leaves
    posl = positions.reshape(3, leaves, width).transpose(1, 0, 2)
    massl = masses.reshape(leaves, width)
    groups = lax.axis_size("grp")
    pairs = leaves * near
    slots = max(2, (2 * pairs + groups - 1) // groups)
    flat = near_src.reshape(pairs)
    owner = flat // leaves
    local = flat % leaves
    target = jnp.arange(pairs, dtype=jnp.int32) // near
    onehot = (owner[:, None] == jnp.arange(groups, dtype=jnp.int32)[None, :]).astype(jnp.int32)
    before = jnp.cumsum(onehot, axis=0) - onehot
    rank = jnp.sum(before * onehot, axis=1)
    slot = owner * slots + rank
    request = jnp.zeros((groups * slots,), jnp.int32).at[slot].set(local).reshape(groups, slots)
    asked = lax.all_to_all(request, "grp", split_axis=0, concat_axis=0, tiled=True)
    got_pos, got_mass = side_by_side((posl[asked], massl[asked]), "grp", 0, 0, 2)
    spos = got_pos.reshape(groups * slots, 3, width)[slot]
    smass = got_mass.reshape(groups * slots, width)[slot]
    per_pair = item_forces(posl[target], spos, smass)
    forces = jnp.sum(per_pair.reshape(leaves, near, 3, width), axis=1)
    accel = forces.transpose(1, 0, 2).reshape(3, -1) * active.astype(jnp.float32)
    cells = multipoles.shape[1]
    coeffs = multipoles.shape[0]
    padded = with_halo(multipoles, (("zone", 1),), cells)
    rows = padded.T[far_src].astype(jnp.float32)
    n_classes = m2l_ops.shape[1] // coeffs
    segment = jnp.arange(cells, dtype=jnp.int32)[:, None] * n_classes + far_class
    sums = jax.ops.segment_sum(
        rows.reshape(-1, coeffs), segment.reshape(-1), num_segments=cells * n_classes
    )
    sums = sums.astype(jnp.bfloat16).reshape(cells, n_classes * coeffs)
    local_coeffs = lax.dot_general(
        m2l_ops, sums, (((1,), (1,)), ((), ())), preferred_element_type=jnp.float32
    )
    return (accel, local_coeffs)


def solution(mesh):
    return jax.shard_map(
        on_device,
        mesh=mesh,
        in_specs=(
            P(None, ("zone", "grp")),
            P(("zone", "grp")),
            P(("zone", "grp")),
            P(("zone", "grp"), None),
            P(None, ("zone", "grp")),
            P(("zone", "grp"), None),
            P(("zone", "grp"), None),
            P(),
        ),
        out_specs=(P(None, ("zone", "grp")), P(None, ("zone", "grp"))),
        check_vma=False,
    )
```

profile of v0, /device:TPU:1, one launch (start us, length us, event | category | flops | bytes accessed | tf_op | source)
XLA Modules:
  0.0 151.9 jit_solution(3016590295604142345)
XLA Ops:
  0.7 0.8 reshape.233
  1.5 0.8 reshape.232
  2.6 0.8 scatter_custom_fusion
  4.2 22.8 %all-to-all-start = ((s32[64,1,2]{2,1,0:T(1,128)}), s32[64,1,2]{2,1,0:T(1,128)S(1)}, u32[]{:S(2)}, u32[]{:S(2)}) async-start(s32[64,1,2]{2,1,0:T(1,128)} %bitcast.8), calls=%async_computation | async-start | bytes 65536 | tf_op jit(solution)/shard_map/all_to_all | solution.py:66
  27.6 12.7 %all-to-all-done = s32[64,1,2]{2,1,0:T(1,128)S(1)} async-done(((s32[64,1,2]{2,1,0:T(1,128)}), s32[64,1,2]{2,1,0:T(1,128)S(1)}, u32[]{:S(2)}, u32[]{:S(2)}) %all-to-all-start) | async-done | bytes 544 | tf_op jit(solution)/shard_map/all_to_all | solution.py:66
  41.5 0.9 gather_fusion
  42.8 1.0 pad_maximum_fusion
  43.9 4.6 %all-to-all-start.1 = ((f32[64,2,1024]{2,1,0:T(2,128)}), f32[64,2,1024]{2,1,0:T(2,128)S(1)}, u32[]{:S(2)}, u32[]{:S(2)}) async-start(f32[64,2,1024]{2,1,0:T(2,128)} %pad_maximum_fusion), calls=%async_computation.1 | async-start | bytes 1048576 | tf_op jit(solution)/shard_map/all_to_all | solution.py:13
  48.5 5.2 %collective-permute-start = (bf16[81,32]{0,1:T(8,128)(2,1)S(1)}, bf16[81,32]{0,1:T(8,128)(2,1)S(1)}, u32[]{:S(2)}, u32[]{:S(2)}) collective-permute-start(bf16[81,32]{0,1:T(8,128)(2,1)S(1)} %copy-done.5), channel_id=1, source_target_pairs={{0,64},{64,128},{128,192},{192,256},{256,320},{320,384},{384,448},... | collective-permute-start | bytes 15560 | tf_op jit(solution)/shard_map/ppermute | solution.py:31
  53.7 1.9 %collective-permute-start.1 = (bf16[81,32]{0,1:T(8,128)(2,1)S(1)}, bf16[81,32]{0,1:T(8,128)(2,1)S(1)}, u32[]{:S(2)}, u32[]{:S(2)}) collective-permute-start(bf16[81,32]{0,1:T(8,128)(2,1)S(1)} %copy-done.5), channel_id=1, source_target_pairs={{64,0},{128,64},{192,128},{256,192},{320,256},{384,320},{448,384},... | collective-permute-start | bytes 15560 | tf_op jit(solution)/shard_map/ppermute | solution.py:32
  56.8 2.1 %collective-permute-done.1 = bf16[81,32]{0,1:T(8,128)(2,1)S(1)} collective-permute-done((bf16[81,32]{0,1:T(8,128)(2,1)S(1)}, bf16[81,32]{0,1:T(8,128)(2,1)S(1)}, u32[]{:S(2)}, u32[]{:S(2)}) %collective-permute-start.1) | collective-permute-done | bytes 5216 | tf_op jit(solution)/shard_map/ppermute | solution.py:32
  59.0 51.1 %scatter_custom_fusion.1 = f32[10112,81]{1,0:T(8,128)} fusion(s32[6048]{0:T(1024)S(1)} %reshape.301, f32[]{:T(128)} %constant.66.clone.1, bf16[96,81]{1,0:T(8,128)(2,1)S(1)} %maximum_bitcast_fusion, s32[6144]{0:T(1024)S(1)} %pad_clamp_fusion), kind=kCustom, calls=%fused_computation.17 | custom fusion | flops 979776 | bytes 3325444 | tf_op jit(solution)/shard_map/scatter-add | solution.py:79
  110.1 2.7 %convert_element_type.20 = bf16[10112,81]{1,0:T(8,128)(2,1)S(1)} convert(f32[10112,81]{1,0:T(8,128)} %scatter_custom_fusion.1) | non-fusion elementwise | flops 819072 | bytes 4914432 | tf_op jit(solution)/shard_map/convert_element_type | solution.py:82
  112.7 2.8 %reshape.241 = bf16[32,25596]{1,0:T(8,128)(2,1)} reshape(bf16[10112,81]{1,0:T(8,128)(2,1)S(1)} %convert_element_type.20) | data formatting | bytes 3276288 | tf_op jit(solution)/shard_map/reshape | solution.py:82
  115.5 4.7 %convolution_bitcast_fusion = f32[81,32]{0,1:T(8,128)} fusion(bf16[32,25596]{1,0:T(8,128)(2,1)} %reshape.241, bf16[81,25596]{1,0:T(8,128)(2,1)} %param.17), kind=kOutput, calls=%fused_computation.20 | convolution fusion | flops 132689664 | bytes 5795064 | tf_op jit(solution)/shard_map/dot_general | solution.py:83
  122.2 29.0 %while.10 = (s32[]{:T(128)}, f32[8,8,3,256]{3,2,1,0:T(4,128)S(1)}, f32[8,8,3,256]{3,2,1,0:T(4,128)S(1)}, f32[8,8,3,256]{3,2,1,0:T(4,128)S(1)}, f32[8,8,256]{2,1,0:T(8,128)S(1)}, /*index=5*/s32[]{:T(128)}) while((s32[]{:T(128)}, f32[8,8,3,256]{3,2,1,0:T(4,128)S(1)}, f32[8,8,3,256]{3,2,1,0:T(4,128)S(1)}, f32[8,8,3,256]{3,2,1,0:T(4,128)S(1)}, ...), condition=%wide.region_6.7_spmd, body=%wide.region_3.6_spmd.sunk | while | flops 10479618 | bytes 8699993 | solution.py:46
  122.2 1.1 fusion.15
  123.9 1.9 %fusion.16 = f32[8,3,256]{2,1,0:T(4,128)S(1)} fusion(f32[8,256,256]{2,1,0:T(8,128)S(1)} %multiply_divide_fusion.2, f32[8,3,256]{2,1,0:T(4,128)S(1)} %get-tuple-element.77, f32[8,3,256]{2,1,0:T(4,128)S(1)} %get-tuple-element.78), kind=kLoop, calls=%fused_computation.11.clone.1 | loop fusion | flops 4712448 | bytes 2170880 | tf_op jit(solution)/shard_map/while/body/eval_jaxpr/vmap()/reduce_sum | solution.py:42
  125.9 1.1 fusion.15
  127.5 1.9 %fusion.16 = f32[8,3,256]{2,1,0:T(4,128)S(1)} fusion(f32[8,256,256]{2,1,0:T(8,128)S(1)} %multiply_divide_fusion.2, f32[8,3,256]{2,1,0:T(4,128)S(1)} %get-tuple-element.77, f32[8,3,256]{2,1,0:T(4,128)S(1)} %get-tuple-element.78), kind=kLoop, calls=%fused_computation.11.clone.1 | loop fusion | flops 4712448 | bytes 2170880 | tf_op jit(solution)/shard_map/while/body/eval_jaxpr/vmap()/reduce_sum | solution.py:42
  129.5 1.1 fusion.15
  131.2 1.9 %fusion.16 = f32[8,3,256]{2,1,0:T(4,128)S(1)} fusion(f32[8,256,256]{2,1,0:T(8,128)S(1)} %multiply_divide_fusion.2, f32[8,3,256]{2,1,0:T(4,128)S(1)} %get-tuple-element.77, f32[8,3,256]{2,1,0:T(4,128)S(1)} %get-tuple-element.78), kind=kLoop, calls=%fused_computation.11.clone.1 | loop fusion | flops 4712448 | bytes 2170880 | tf_op jit(solution)/shard_map/while/body/eval_jaxpr/vmap()/reduce_sum | solution.py:42
  133.1 1.1 fusion.15
  134.8 1.9 %fusion.16 = f32[8,3,256]{2,1,0:T(4,128)S(1)} fusion(f32[8,256,256]{2,1,0:T(8,128)S(1)} %multiply_divide_fusion.2, f32[8,3,256]{2,1,0:T(4,128)S(1)} %get-tuple-element.77, f32[8,3,256]{2,1,0:T(4,128)S(1)} %get-tuple-element.78), kind=kLoop, calls=%fused_computation.11.clone.1 | loop fusion | flops 4712448 | bytes 2170880 | tf_op jit(solution)/shard_map/while/body/eval_jaxpr/vmap()/reduce_sum | solution.py:42
  136.8 1.1 fusion.15
  138.4 1.9 %fusion.16 = f32[8,3,256]{2,1,0:T(4,128)S(1)} fusion(f32[8,256,256]{2,1,0:T(8,128)S(1)} %multiply_divide_fusion.2, f32[8,3,256]{2,1,0:T(4,128)S(1)} %get-tuple-element.77, f32[8,3,256]{2,1,0:T(4,128)S(1)} %get-tuple-element.78), kind=kLoop, calls=%fused_computation.11.clone.1 | loop fusion | flops 4712448 | bytes 2170880 | tf_op jit(solution)/shard_map/while/body/eval_jaxpr/vmap()/reduce_sum | solution.py:42
  140.4 1.1 fusion.15
  142.1 1.9 %fusion.16 = f32[8,3,256]{2,1,0:T(4,128)S(1)} fusion(f32[8,256,256]{2,1,0:T(8,128)S(1)} %multiply_divide_fusion.2, f32[8,3,256]{2,1,0:T(4,128)S(1)} %get-tuple-element.77, f32[8,3,256]{2,1,0:T(4,128)S(1)} %get-tuple-element.78), kind=kLoop, calls=%fused_computation.11.clone.1 | loop fusion | flops 4712448 | bytes 2170880 | tf_op jit(solution)/shard_map/while/body/eval_jaxpr/vmap()/reduce_sum | solution.py:42
  144.0 1.1 fusion.15
  145.7 1.9 %fusion.16 = f32[8,3,256]{2,1,0:T(4,128)S(1)} fusion(f32[8,256,256]{2,1,0:T(8,128)S(1)} %multiply_divide_fusion.2, f32[8,3,256]{2,1,0:T(4,128)S(1)} %get-tuple-element.77, f32[8,3,256]{2,1,0:T(4,128)S(1)} %get-tuple-element.78), kind=kLoop, calls=%fused_computation.11.clone.1 | loop fusion | flops 4712448 | bytes 2170880 | tf_op jit(solution)/shard_map/while/body/eval_jaxpr/vmap()/reduce_sum | solution.py:42
  147.6 1.1 fusion.15
  149.3 1.9 %fusion.16 = f32[8,3,256]{2,1,0:T(4,128)S(1)} fusion(f32[8,256,256]{2,1,0:T(8,128)S(1)} %multiply_divide_fusion.2, f32[8,3,256]{2,1,0:T(4,128)S(1)} %get-tuple-element.77, f32[8,3,256]{2,1,0:T(4,128)S(1)} %get-tuple-element.78), kind=kLoop, calls=%fused_computation.11.clone.1 | loop fusion | flops 4712448 | bytes 2170880 | tf_op jit(solution)/shard_map/while/body/eval_jaxpr/vmap()/reduce_sum | solution.py:42
  (82 shorter events, 11.9 us)
Async XLA Ops:
  0.6 40.9 %copy-start = (f32[3,2048]{1,0:T(4,128)S(1)}, f32[3,2048]{1,0:T(4,128)}, u32[]{:S(2)}) copy-start(f32[3,2048]{1,0:T(4,128)} %param.10) | copy-start | bytes 73732
  0.6 47.9 %copy-start.5 = (bf16[81,32]{0,1:T(8,128)(2,1)S(1)}, bf16[81,32]{0,1:T(8,128)(2,1)}, u32[]{:S(2)}) copy-start(bf16[81,32]{0,1:T(8,128)(2,1)} %param.14) | copy-start | bytes 15556
  0.7 55.0 %copy-start.2 = (s32[32,189]{1,0:T(8,128)S(1)}, s32[32,189]{1,0:T(8,128)}, u32[]{:S(2)}) copy-start(s32[32,189]{1,0:T(8,128)} %param.15) | copy-start | bytes 72580
  0.7 55.2 %copy-start.3 = (s32[32,189]{1,0:T(8,128)S(1)}, s32[32,189]{1,0:T(8,128)}, u32[]{:S(2)}) copy-start(s32[32,189]{1,0:T(8,128)} %param.16) | copy-start | bytes 72580
  2.2 53.7 %copy-start.4 = (s32[2048]{0:T(1024)S(1)}, s32[2048]{0:T(1024)}, u32[]{:S(2)}) copy-start(s32[2048]{0:T(1024)} %param.12) | copy-start | bytes 24580
  4.2 36.2 %all-to-all-start = ((s32[64,1,2]{2,1,0:T(1,128)}), s32[64,1,2]{2,1,0:T(1,128)S(1)}, u32[]{:S(2)}, u32[]{:S(2)}) async-start(s32[64,1,2]{2,1,0:T(1,128)} %bitcast.8), calls=%async_computation | async-start | bytes 65536 | tf_op jit(solution)/shard_map/all_to_all | solution.py:66
  43.9 76.4 %all-to-all-start.1 = ((f32[64,2,1024]{2,1,0:T(2,128)}), f32[64,2,1024]{2,1,0:T(2,128)S(1)}, u32[]{:S(2)}, u32[]{:S(2)}) async-start(f32[64,2,1024]{2,1,0:T(2,128)} %pad_maximum_fusion), calls=%async_computation.1 | async-start | bytes 1048576 | tf_op jit(solution)/shard_map/all_to_all | solution.py:13
  48.5 8.3 %collective-permute-start = (bf16[81,32]{0,1:T(8,128)(2,1)S(1)}, bf16[81,32]{0,1:T(8,128)(2,1)S(1)}, u32[]{:S(2)}, u32[]{:S(2)}) collective-permute-start(bf16[81,32]{0,1:T(8,128)(2,1)S(1)} %copy-done.5), channel_id=1, source_target_pairs={{0,64},{64,128},{128,192},{192,256},{256,320},{320,384},{384,448},... | collective-permute-start | bytes 15560 | tf_op jit(solution)/shard_map/ppermute | solution.py:31
  53.7 5.3 %collective-permute-start.1 = (bf16[81,32]{0,1:T(8,128)(2,1)S(1)}, bf16[81,32]{0,1:T(8,128)(2,1)S(1)}, u32[]{:S(2)}, u32[]{:S(2)}) collective-permute-start(bf16[81,32]{0,1:T(8,128)(2,1)S(1)} %copy-done.5), channel_id=1, source_target_pairs={{64,0},{128,64},{192,128},{256,192},{320,256},{384,320},{448,384},... | collective-permute-start | bytes 15560 | tf_op jit(solution)/shard_map/ppermute | solution.py:32
  120.2 2.0 %copy-start.1 = (f32[8,8,3,256]{3,2,1,0:T(4,128)S(1)}, f32[8,8,3,256]{3,2,1,0:T(4,128)}, u32[]{:S(2)}) copy-start(f32[8,8,3,256]{3,2,1,0:T(4,128)} %custom-call.12) | copy-start | bytes 589828
where the time goes:
time: 154 us; the launch traced here: 152 us
  other arithmetic  84.2 us (55%)
  starting transfers between devices  34.5 us (22%)
  waiting for transfers between devices  14.8 us (10%)
  local copies, waits for them, and re-layouts  12.3 us (8%)
  matrix products  4.69 us (3%)
    scatter-add x1, other arithmetic, on_device(): jax.ops.segment_sum(rows.reshape(-1, coeffs), segment.reshape(-1), num_se...  51.1 us
    all_to_all x1, starting transfers between devices, on_device(): lax.all_to_all(request, 'grp', split_axis=0, concat_axis=0, tiled=True)  22.8 us
    reduce_sum x8, other arithmetic, one_pair(): return jnp.sum(delta * weight[None], axis=2)  14.9 us
    all_to_all x1, waiting for transfers between devices, on_device(): lax.all_to_all(request, 'grp', split_axis=0, concat_axis=0, tiled=True)  12.7 us
    reduce_sum x8, other arithmetic, one_pair(): dist2 = jnp.sum(delta * delta, axis=0) + softening  8.85 us
    ppermute x1, starting transfers between devices, with_halo(): before = lax.ppermute(last, axis, up)  5.19 us
    dot_general x1, matrix products, on_device(): lax.dot_general(m2l_ops, sums, (((1,), (1,)), ((), ())), preferred_elemen...  4.69 us
    all_to_all x1, starting transfers between devices, side_by_side(): lax.all_to_all(both, axis, split_axis=split_dim, concat_axis=concat_dim,...  4.63 us
  transfers between devices with their start and end apart: 4, of which 2 were waited for; matrix products, arithmetic and copies ran while one was open for 41% of the time, Pallas kernels for 0%

commit v1 on v0

v1 whole, which is shorter than its diff:
```python
import functools
import jax
import jax.numpy as jnp
from jax import lax
from jax.experimental import pallas as pl
from jax.experimental.pallas import tpu as pltpu
from jax.sharding import PartitionSpec as P

F32, BF16, I32 = jnp.float32, jnp.bfloat16, jnp.int32
SOFT = 0.0025
NT = (((1,), (1,)), ((), ()))
NN = (((1,), (0,)), ((), ()))


def dot(a, b, dims=NN):
    return lax.dot_general(a, b, dims, preferred_element_type=F32)


def packed(x, y, z, m):
    def q(v):
        return jnp.minimum((v * 65536.0).astype(I32), 65535) - 32768

    mass = jnp.minimum((m * 4194304.0 + 0.5).astype(I32), 65535)
    return (q(x) << 16) | (q(y) & 65535), (q(z) << 16) | mass


def features(w0, w1):
    row = lax.broadcasted_iota(I32, w0.shape, 0)
    comp = jnp.where(row < 3, row, row - 3)
    w = jnp.where(comp == 2, w1, w0)
    up = jnp.where(comp == 1, 16, 0)
    high = (w << up) >> 24
    low = lax.shift_right_logical(w << (up + 8), 24)
    part = jnp.where(
        row < 3, high.astype(F32) * (1.0 / 256), low.astype(F32) * (1.0 / 65536)
    )
    swap = jnp.where(
        row < 3, low.astype(F32) * (1.0 / 65536), high.astype(F32) * (1.0 / 256)
    )
    part = jnp.where(row < 6, part, 0.0)
    swap = jnp.where(row < 6, swap, 0.0)
    px = (w0 >> 16).astype(F32) * (1.0 / 65536)
    py = ((w0 << 16) >> 16).astype(F32) * (1.0 / 65536)
    pz = (w1 >> 16).astype(F32) * (1.0 / 65536)
    mass = (w1 & 65535).astype(F32) * (1.0 / 4194304)
    norm = px * px + py * py + pz * pz
    return row, part, swap, px, py, pz, mass, norm


def three(v):
    a = v.astype(BF16).astype(F32)
    b = (v - a).astype(BF16).astype(F32)
    c = v - a - b
    return a, b, c


def source_rows(w0, w1):
    row, part, _, px, py, pz, mass, norm = features(w0, w1)
    a, b, c = three(norm)
    extra = jnp.where(row == 0, a, jnp.where(row == 1, b, jnp.where(row == 2, c, jnp.where(row < 6, 1.0, 0.0))))
    s = jnp.concatenate([part, part, extra, jnp.zeros_like(part)], axis=0).astype(BF16)
    q = row & 3
    v = mass * jnp.where(q == 0, px, jnp.where(q == 1, py, jnp.where(q == 2, pz, 1.0)))
    hi = v.astype(BF16).astype(F32)
    b = jnp.where(row < 4, hi, v - hi).astype(BF16)
    return s, b


def target_rows(w0, w1):
    row, part, swap, px, py, pz, mass, norm = features(w0, w1)
    a, b, c = three(norm + SOFT)
    extra = jnp.where(row < 3, 1.0, jnp.where(row == 3, a, jnp.where(row == 4, b, jnp.where(row == 5, c, 0.0))))
    t = jnp.concatenate([part * -2.0, swap * -2.0, extra, jnp.zeros_like(part)], axis=0)
    return t, px[0:1], py[0:1], pz[0:1]


def words(ref, leaf, width):
    w = ref[leaf]
    return (
        jnp.broadcast_to(w[0:1], (8, width)),
        jnp.broadcast_to(w[1:2], (8, width)),
    )


def near_kernel(leaves, near, width, idx_ref, table_ref, own_ref, act_ref, out_ref):
    def one_leaf(t, carry):
        tgt, px, py, pz = target_rows(*words(own_ref, t, width))
        tt = jnp.transpose(tgt).astype(BF16)
        acc = jnp.zeros((width, 8), F32)
        for s in range(near):
            leaf = idx_ref[t * near + s]
            rows, b = source_rows(*words(table_ref, leaf, width))
            d = dot(tt, rows)
            r = lax.rsqrt(d)
            w = (r * r * r).astype(BF16)
            acc = acc + dot(w, b, NT)
        f = jnp.transpose(acc)
        f = f[0:4] + f[4:8]
        m = f[3:4]
        act = act_ref[pl.ds(t, 1), :].astype(F32)
        res = jnp.concatenate([(f[0:1] - px * m), (f[1:2] - py * m), (f[2:3] - pz * m)], axis=0) * act
        out_ref[:, pl.ds(pl.multiple_of(t * width, width), width)] = res
        return carry

    lax.fori_loop(0, leaves, one_leaf, 0)


def near_call(idx, table, own, act):
    leaves, _, width = own.shape
    near = idx.shape[0] // leaves
    return pl.pallas_call(
        functools.partial(near_kernel, leaves, near, width),
        out_shape=jax.ShapeDtypeStruct((3, leaves * width), F32),
        in_specs=[pl.BlockSpec(memory_space=pltpu.SMEM)]
        + [pl.BlockSpec(memory_space=pltpu.VMEM)] * 3,
        out_specs=pl.BlockSpec(memory_space=pltpu.VMEM),
    )(idx, table, own, act)


def place(c):
    return (c & ~63) | ((c & 7) << 3) | ((c >> 3) & 7)


def m2l_kernel(cells, coeffs, classes, cpad, kpad, src_ref, cls_ref, mp_ref, ops_ref, out_ref, src_s, cls_s, r_s, g_s):
    far = src_ref.shape[1]
    src_s[...] = jnp.full(src_s.shape, -1, I32)
    cls_s[...] = jnp.full(cls_s.shape, -1, I32)
    src_s[:, 0:far] = src_ref[...]
    cls_s[:, 0:far] = place(cls_ref[...])
    rows = (coeffs + 15) // 16 * 16
    mp = jnp.concatenate([mp_ref[...].astype(F32), jnp.zeros((rows - coeffs, mp_ref.shape[1]), F32)], axis=0).astype(BF16)
    nsrc = mp.shape[1]
    r_s[...] = jnp.zeros(r_s.shape, BF16)

    def gather_cells(i, carry):
        for u in range(UR):
            t = i * UR + u
            src = src_s[pl.ds(t, 1), :]
            pick = (lax.broadcasted_iota(I32, (nsrc, kpad), 0) == src).astype(F32).astype(BF16)
            r_s[t, 0:rows, :] = dot(mp, pick).astype(BF16)
        return carry

    lax.fori_loop(0, cells // UR, gather_cells, 0)

    def one_cell(t):
        cls = cls_s[pl.ds(t, 1), :]
        hot = (lax.broadcasted_iota(I32, (cpad, kpad), 0) == cls).astype(F32).astype(BF16)
        g = dot(hot, r_s[t], NT)
        for v in range(cpad // 8):
            part = g[8 * v : 8 * v + 8]
            shift, stride = (64 * (v // 8) + v % 8) * coeffs % 128, 8 * coeffs % 128
            if shift + 7 * stride >= 128:
                part = pltpu.roll(part, shift, 1)
                shift = 0
            part = pltpu.roll(part, shift, 1, stride=stride, stride_axis=0)
            g_s[pl.ds(t + 8 * v * cells, 8, stride=cells), :] = part

    def some_cells(i, carry):
        for u in range(UG):
            one_cell(i * UG + u)
        return carry

    lax.fori_loop(0, cells // UG, some_cells, 0)
    lane = lax.broadcasted_iota(I32, (cells, 128), 1)
    tiles = (coeffs * classes + 127) // 128
    whole = coeffs * classes // 128

    def rows_of(c):
        return g_s[pl.ds(pl.multiple_of(place(c) * cells, cells), cells), :]

    def values(q):
        c = q * 128 // coeffs
        edge = (c + 1) * coeffs - q * 128
        x = jnp.where(lane < edge, rows_of(c), rows_of(jnp.minimum(c + 1, classes - 1)))
        x = jnp.where(lane < edge + coeffs, x, rows_of(jnp.minimum(c + 2, classes - 1)))
        return x.astype(BF16)

    def step(i, acc):
        for u in range(0, UF, 2):
            q = i * UF + u
            o = ops_ref[:, pl.ds(pl.multiple_of(q * 128, 256), 256)]
            acc = acc + dot(o, jnp.concatenate([values(q), values(q + 1)], axis=1), NT)
        return acc

    main = (tiles - 1) // UF
    acc = lax.fori_loop(0, main, step, jnp.zeros((coeffs, cells), F32))
    for q in range(main * UF, tiles):
        end = min(q * 128 + 128, coeffs * classes)
        o = ops_ref[:, q * 128 : end]
        x = values(jnp.int32(q))
        if end < q * 128 + 128:
            o = jnp.concatenate([o, jnp.zeros((coeffs, q * 128 + 128 - end), o.dtype)], axis=1)
            x = jnp.where(lane < end - q * 128, x.astype(F32), 0.0).astype(BF16)
        acc = acc + dot(o, x, NT)
    out_ref[...] = acc


UR, UG, UF = 4, 4, 8


def m2l_call(src, cls, mp, ops):
    cells, far = src.shape
    coeffs = mp.shape[0]
    classes = ops.shape[1] // coeffs
    cpad = (classes + 63) // 64 * 64
    kpad = (far + 127) // 128 * 128
    return pl.pallas_call(
        functools.partial(m2l_kernel, cells, coeffs, classes, cpad, kpad),
        out_shape=jax.ShapeDtypeStruct((coeffs, cells), F32),
        in_specs=[pl.BlockSpec(memory_space=pltpu.VMEM)] * 4,
        out_specs=pl.BlockSpec(memory_space=pltpu.VMEM),
        scratch_shapes=[
            pltpu.VMEM((cells, kpad), I32),
            pltpu.VMEM((cells, kpad), I32),
            pltpu.VMEM((cells, 128, kpad), BF16),
            pltpu.VMEM((cpad * cells, 128), F32),
        ],
        compiler_params=pltpu.CompilerParams(vmem_limit_bytes=48 * 1024 * 1024),
        cost_estimate=pl.CostEstimate(flops=10**10, bytes_accessed=5 * 10**6, transcendentals=0),
    )(src, cls, mp, ops)


def on_device(positions, masses, active, near_src, multipoles, far_src, far_class, m2l_ops):
    leaves, near = near_src.shape
    width = positions.shape[1] // leaves
    w0, w1 = packed(positions[0], positions[1], positions[2], masses)
    own = jnp.stack([w0.reshape(leaves, width), w1.reshape(leaves, width)], axis=1)
    table = lax.all_gather(own, "grp", axis=0, tiled=True)
    zones = lax.axis_size("zone")
    up = [(i, i + 1) for i in range(zones - 1)]
    down = [(i + 1, i) for i in range(zones - 1)]
    before = lax.ppermute(multipoles, "zone", up)
    after = lax.ppermute(multipoles, "zone", down)
    local = m2l_call(far_src, far_class, jnp.concatenate([before, multipoles, after], axis=1), m2l_ops)
    accel = near_call(near_src.reshape(-1), table, own, active.reshape(leaves, width))
    return accel, local


def solution(mesh):
    return jax.shard_map(
        on_device,
        mesh=mesh,
        in_specs=(
            P(None, ("zone", "grp")),
            P(("zone", "grp")),
            P(("zone", "grp")),
            P(("zone", "grp"), None),
            P(None, ("zone", "grp")),
            P(("zone", "grp"), None),
            P(("zone", "grp"), None),
            P(),
        ),
        out_specs=(P(None, ("zone", "grp")), P(None, ("zone", "grp"))),
        check_vma=False,
    )
```

time: 154 us -> 184 us (1.19)
  the two profiles are of different devices: /device:TPU:1 before, /device:TPU:8 now
where the time goes in v1:
time: 184 us; the launch traced here: 183 us
  waiting for transfers between devices  130 us (71%)
  Pallas kernels  24.1 us (13%)
  between operations  14.1 us (8%)
  local copies, waits for them, and re-layouts  7.88 us (4%)
  starting transfers between devices  4.36 us (2%)
  other arithmetic  2.34 us (1%)
    all_gather x1, waiting for transfers between devices, on_device(): table = lax.all_gather(own, 'grp', axis=0, tiled=True)  119 us
    pallas_call x1, Pallas kernels, m2l_call(): pl.pallas_call(functools.partial(m2l_kernel, cells, coeffs, classes, cpad...  14.3 us
    ppermute x1, waiting for transfers between devices, on_device(): before = lax.ppermute(multipoles, 'zone', up)  11.5 us
    pallas_call x1, Pallas kernels, near_call(): pl.pallas_call(functools.partial(near_kernel, leaves, near, width), out_s...  9.75 us
    unnamed x8, local copies, waits for them, and re-layouts  5.28 us
  transfers between devices with their start and end apart: 3, of which 2 were waited for; matrix products, arithmetic and copies ran while one was open for 2% of the time, Pallas kernels for 8%

profile of v1, /device:TPU:8, one launch (start us, length us, event | category | flops | bytes accessed | tf_op | source)
XLA Modules:
  0.0 183.2 jit_solution(17208013312048425547)
XLA Ops:
  7.2 0.0 all-gather.2.cloned.1.call-start
  7.2 0.9 and_or_fusion
  8.1 0.7 minimum_or_fusion
  8.8 0.6 pad_add_fusion.own_ref
  9.5 0.0 all-gather.2.cloned.1.call-update
  9.5 0.8 copy.14
  10.3 1.9 %collective-permute-start.1 = (bf16[81,32]{1,0:T(8,128)(2,1)S(1)}, bf16[81,32]{1,0:T(8,128)(2,1)S(1)}, u32[]{:S(2)}, u32[]{:S(2)}) collective-permute-start(bf16[81,32]{1,0:T(8,128)(2,1)S(1)} %copy.14), channel_id=1, source_target_pairs={{64,0},{128,64},{192,128},{256,192},{320,256},{384,320},{448,384},... | collective-permute-start | bytes 15560 | tf_op jit(solution)/shard_map/ppermute | solution.py:233
  12.2 2.4 %collective-permute-start = (bf16[81,32]{1,0:T(8,128)(2,1)S(1)}, bf16[81,32]{1,0:T(8,128)(2,1)S(1)}, u32[]{:S(2)}, u32[]{:S(2)}) collective-permute-start(bf16[81,32]{1,0:T(8,128)(2,1)S(1)} %copy.14), channel_id=1, source_target_pairs={{0,64},{64,128},{128,192},{192,256},{256,320},{320,384},{384,448},... | collective-permute-start | bytes 15560 | tf_op jit(solution)/shard_map/ppermute | solution.py:232
  14.6 1.3 reshape.78.idx_ref
  15.9 1.3 reshape.79.act_ref
  17.2 0.0 collective-permute-done.1
  17.2 11.5 %collective-permute-done = bf16[81,32]{1,0:T(8,128)(2,1)S(1)} collective-permute-done((bf16[81,32]{1,0:T(8,128)(2,1)S(1)}, bf16[81,32]{1,0:T(8,128)(2,1)S(1)}, u32[]{:S(2)}, u32[]{:S(2)}) %collective-permute-start) | collective-permute-done | bytes 5216 | tf_op jit(solution)/shard_map/ppermute | solution.py:232
  28.8 0.1 pad_maximum_fusion.mp_ref
  28.9 0.0 copy-start
  28.9 2.3 %copy-done = bf16[81,25596]{1,0:T(8,128)(2,1)S(1)} copy-done((bf16[81,25596]{1,0:T(8,128)(2,1)S(1)}, bf16[81,25596]{1,0:T(8,128)(2,1)}, u32[]{:S(2)}) %copy-start) | copy-done | bytes 4146576
  31.2 0.0 copy-start.1
  31.2 0.8 copy-done.1
  31.9 0.0 copy-start.2
  31.9 0.8 copy-done.2
  32.7 14.3 %shard_map.96 = f32[81,32]{1,0:T(8,128)S(1)} custom-call(s32[32,189]{1,0:T(8,128)S(1)} %copy-done.1, s32[32,189]{1,0:T(8,128)S(1)} %copy-done.2, bf16[81,96]{1,0:T(8,128)(2,1)S(1)} %pad_maximum_fusion.mp_ref, bf16[81,25596]{1,0:T(8,128)(2,1)S(1)} %copy-done), custom_call_target="tpu_custom_call" | custom-call | flops 10000000000 | bytes 5000000 | tf_op jit(solution)/shard_map/pallas_call | solution.py:207
  47.0 0.7 copy.17
  47.7 118.9 %all-gather.2.cloned.1.call-done.table_ref = s32[512,2,256]{2,1,0:T(2,128)} async-done(((s32[8,2,256]{2,1,0:T(2,128)}), s32[512,2,256]{2,1,0:T(2,128)}) %all-gather.2.cloned.1.call-update) | async-done | bytes 1048592 | tf_op jit(solution)/shard_map/all_gather | solution.py:228
  166.6 9.8 %shard_map.95 = f32[3,2048]{1,0:T(4,128)} custom-call(s32[64]{0:T(128)} %reshape.78.idx_ref, s32[512,2,256]{2,1,0:T(2,128)} %all-gather.2.cloned.1.call-done.table_ref, s32[8,2,256]{2,1,0:T(2,128)} %pad_add_fusion.own_ref, s32[8,256]{1,0:T(8,128)} %reshape.79.act_ref), custom_call_target="tpu_custom_call" | custom-call | tf_op jit(solution)/shard_map/pallas_call | solution.py:111
Async XLA Ops:
  7.2 159.4 %all-gather.2.cloned.1.call-start = ((), (), s32[]{:S(2)}) async-start(), calls=%async_computation | async-start | bytes 1064960 | tf_op jit(solution)/shard_map/all_gather | solution.py:228
  10.3 6.9 %collective-permute-start.1 = (bf16[81,32]{1,0:T(8,128)(2,1)S(1)}, bf16[81,32]{1,0:T(8,128)(2,1)S(1)}, u32[]{:S(2)}, u32[]{:S(2)}) collective-permute-start(bf16[81,32]{1,0:T(8,128)(2,1)S(1)} %copy.14), channel_id=1, source_target_pairs={{64,0},{128,64},{192,128},{256,192},{320,256},{384,320},{448,384},... | collective-permute-start | bytes 15560 | tf_op jit(solution)/shard_map/ppermute | solution.py:233
  12.2 16.6 %collective-permute-start = (bf16[81,32]{1,0:T(8,128)(2,1)S(1)}, bf16[81,32]{1,0:T(8,128)(2,1)S(1)}, u32[]{:S(2)}, u32[]{:S(2)}) collective-permute-start(bf16[81,32]{1,0:T(8,128)(2,1)S(1)} %copy.14), channel_id=1, source_target_pairs={{0,64},{64,128},{128,192},{192,256},{256,320},{320,384},{384,448},... | collective-permute-start | bytes 15560 | tf_op jit(solution)/shard_map/ppermute | solution.py:232
  28.9 2.3 %copy-start = (bf16[81,25596]{1,0:T(8,128)(2,1)S(1)}, bf16[81,25596]{1,0:T(8,128)(2,1)}, u32[]{:S(2)}) copy-start(bf16[81,25596]{1,0:T(8,128)(2,1)} %ops_ref.1) | copy-start | bytes 12439660
  31.2 0.8 copy-start.1
  31.9 0.8 copy-start.2
Sparse Core Ops, SparseCore 0:
  12.1 154.4 all-gather.1

commit v2 on v1

v2 whole, which is shorter than its diff:
```python
import functools
import jax
import jax.numpy as jnp
from jax import lax
from jax.experimental import pallas as pl
from jax.experimental.pallas import tpu as pltpu
from jax.sharding import PartitionSpec as P

F32, BF16, I32 = jnp.float32, jnp.bfloat16, jnp.int32
SOFT = 0.0025
NT = (((1,), (1,)), ((), ()))
NN = (((1,), (0,)), ((), ()))


def dot(a, b, dims=NN):
    return lax.dot_general(a, b, dims, preferred_element_type=F32)


def packed(x, y, z, m):
    def q(v):
        return jnp.minimum((v * 65536.0).astype(I32), 65535) - 32768

    mass = jnp.minimum((m * 4194304.0 + 0.5).astype(I32), 65535)
    return (q(x) << 16) | (q(y) & 65535), (q(z) << 16) | mass


def features(w0, w1):
    row = lax.broadcasted_iota(I32, w0.shape, 0)
    comp = jnp.where(row < 3, row, row - 3)
    w = jnp.where(comp == 2, w1, w0)
    up = jnp.where(comp == 1, 16, 0)
    high = (w << up) >> 24
    low = lax.shift_right_logical(w << (up + 8), 24)
    part = jnp.where(
        row < 3, high.astype(F32) * (1.0 / 256), low.astype(F32) * (1.0 / 65536)
    )
    swap = jnp.where(
        row < 3, low.astype(F32) * (1.0 / 65536), high.astype(F32) * (1.0 / 256)
    )
    part = jnp.where(row < 6, part, 0.0)
    swap = jnp.where(row < 6, swap, 0.0)
    px = (w0 >> 16).astype(F32) * (1.0 / 65536)
    py = ((w0 << 16) >> 16).astype(F32) * (1.0 / 65536)
    pz = (w1 >> 16).astype(F32) * (1.0 / 65536)
    mass = (w1 & 65535).astype(F32) * (1.0 / 4194304)
    norm = px * px + py * py + pz * pz
    return row, part, swap, px, py, pz, mass, norm


def three(v):
    a = v.astype(BF16).astype(F32)
    b = (v - a).astype(BF16).astype(F32)
    c = v - a - b
    return a, b, c


def source_rows(w0, w1):
    row, part, _, px, py, pz, mass, norm = features(w0, w1)
    a, b, c = three(norm)
    extra = jnp.where(row == 0, a, jnp.where(row == 1, b, jnp.where(row == 2, c, jnp.where(row < 6, 1.0, 0.0))))
    s = jnp.concatenate([part, part, extra, jnp.zeros_like(part)], axis=0).astype(BF16)
    q = row & 3
    v = mass * jnp.where(q == 0, px, jnp.where(q == 1, py, jnp.where(q == 2, pz, 1.0)))
    hi = v.astype(BF16).astype(F32)
    b = jnp.where(row < 4, hi, v - hi).astype(BF16)
    return s, b


def target_rows(w0, w1):
    row, part, swap, px, py, pz, mass, norm = features(w0, w1)
    a, b, c = three(norm + SOFT)
    extra = jnp.where(row < 3, 1.0, jnp.where(row == 3, a, jnp.where(row == 4, b, jnp.where(row == 5, c, 0.0))))
    t = jnp.concatenate([part * -2.0, swap * -2.0, extra, jnp.zeros_like(part)], axis=0)
    return t, px[0:1], py[0:1], pz[0:1]


def words(ref, leaf, width):
    w = ref[leaf]
    return (
        jnp.broadcast_to(w[0:1], (8, width)),
        jnp.broadcast_to(w[1:2], (8, width)),
    )


def place(c):
    return (c & ~63) | ((c & 7) << 3) | ((c >> 3) & 7)


def kernel(cfg, pos_h, mass_h, act_h, near_h, mp_h, src_h, cls_h, ops_h, acc_o, loc_o,
           pos_v, mass_v, act_v, idx_s, mp_v, src_v, cls_v, ops_v, table, src_s, cls_s, mp_s, r_s, g_s,
           in_sem, halo_send, halo_recv, z_send, z_recv, x_send, x_recv):
    leaves, near, width, cells, far, coeffs, classes, cpad, kpad, zones, X, Z, R = cfg
    zone, g = lax.axis_index("zone"), lax.axis_index("grp")
    z, x = g // X, g % X
    plus, minus = Z // 2, Z - 1 - Z // 2

    def grp_at(dz, dx):
        return lax.rem(z + dz + 2 * Z, Z) * X + lax.rem(x + dx + X, X)

    def zone_at(d):
        return lax.rem(zone + d + zones, zones)

    barrier = pltpu.get_barrier_semaphore()
    reach = [d for r in range(1, R + 1) for d in (r, -r)]
    if 2 * R == Z:
        reach.remove(-R)
    peers = [{"grp": grp_at(d, 0)} for d in reach] + [{"grp": grp_at(0, d)} for d in range(1, X)]
    peers += [{"zone": zone_at(1)}, {"zone": zone_at(-1)}]
    for peer in peers:
        pl.semaphore_signal(barrier, inc=1, device_id=peer, device_id_type=MESH)

    loads = [
        pltpu.make_async_copy(a, b, in_sem.at[n])
        for n, (a, b) in enumerate(
            [(pos_h, pos_v), (mass_h, mass_v), (mp_h, mp_v.at[1]), (src_h, src_v), (cls_h, cls_v), (near_h, idx_s), (act_h, act_v), (ops_h, ops_v)]
        )
    ]
    for load in loads:
        load.start()

    loads[0].wait()
    loads[1].wait()
    own = g * leaves
    lanes = mass_v.shape[1]
    per = width // lanes
    for l in range(leaves):
        at = slice(l * width, (l + 1) * width)
        mass = jnp.concatenate([mass_v[per * l + k : per * l + k + 1, :] for k in range(per)], axis=1)
        w0, w1 = packed(pos_v[0:1, at], pos_v[1:2, at], pos_v[2:3, at], mass)
        table[own + l, 0:1, :] = w0
        table[own + l, 1:2, :] = w1
    loads[2].wait()
    pl.semaphore_wait(barrier, len(peers))

    halo = [
        pltpu.make_async_remote_copy(
            src_ref=mp_v.at[1], dst_ref=mp_v.at[1 - d], send_sem=halo_send.at[n], recv_sem=halo_recv.at[n],
            device_id={"zone": zone_at(d)}, device_id_type=MESH)
        for n, d in enumerate((1, -1))
    ]

    def block(o, dx=0):
        return table.at[pl.ds(grp_at(-o, dx) * leaves, leaves)]

    def z_copy(o, d):
        n = (o + d) % Z
        return pltpu.make_async_remote_copy(
            src_ref=block(o), dst_ref=block(o), send_sem=z_send.at[n], recv_sem=z_recv.at[n],
            device_id={"grp": grp_at(d, 0)}, device_id_type=MESH)

    def x_copy(o, dx):
        n = (dx - 1) * Z + o % Z
        return pltpu.make_async_remote_copy(
            src_ref=block(o), dst_ref=block(o), send_sem=x_send.at[n], recv_sem=x_recv.at[n],
            device_id={"grp": grp_at(0, dx)}, device_id_type=MESH)

    def z_wait(o):
        n = o % Z
        pltpu.make_async_remote_copy(
            src_ref=block(o), dst_ref=block(o), send_sem=z_send.at[n], recv_sem=z_recv.at[n],
            device_id={"grp": grp_at(1, 0)}, device_id_type=MESH).wait_recv()

    def x_wait(o, dx):
        n = (dx - 1) * Z + o % Z
        pltpu.make_async_remote_copy(
            src_ref=block(o, -dx), dst_ref=block(o, -dx), send_sem=x_send.at[n], recv_sem=x_recv.at[n],
            device_id={"grp": grp_at(0, dx)}, device_id_type=MESH).wait_recv()

    dxs = [d for d in (1, 3, 2) if d < X]
    sent = []

    def send(make, *at):
        make(*at).start()
        sent.append((make, at))

    for h in halo:
        h.start()
    for d in reversed(reach):
        send(z_copy, 0, d)
    for dx in dxs:
        send(x_copy, 0, dx)

    def arrived(o):
        z_wait(o)
        if o == R:
            for d in range(plus - R, 0, -1):
                send(z_copy, o, d)
        if o == -R:
            for d in range(minus - R, 0, -1):
                send(z_copy, o, -d)
        for dx in dxs:
            send(x_copy, o, dx)

    events = {}
    groups = cells // UG
    order = [o for r in range(1, plus + 1) for o in (r, -r) if o <= plus and -o <= minus]
    for o in order:
        a = abs(o)
        where = ("g", EV_G[a]) if a in EV_G else ("f", EV_F[a])
        events.setdefault(where, []).append(o)

    def run_events(kind, i, n):
        for k in range(n):
            if (kind, k) in events:
                @pl.when(i == k)
                def _():
                    for o in events[(kind, k)]:
                        arrived(o)

    loads[3].wait()
    loads[4].wait()
    src_s[...] = jnp.full(src_s.shape, -1, I32)
    cls_s[...] = jnp.full(cls_s.shape, -1, I32)
    src_s[:, 0:far] = src_v[...]
    cls_s[:, 0:far] = place(cls_v[...])
    mp_s[...] = jnp.zeros(mp_s.shape, F32)
    for h in halo:
        h.wait_recv()
    keep = [(zone > 0).astype(F32), 1.0, (zone < zones - 1).astype(F32)]
    for d in range(3):
        mp_s[d * cells : (d + 1) * cells, 0:coeffs] = mp_v[d].astype(F32) * keep[d]
    mp = jnp.transpose(mp_s[...]).astype(BF16)
    nsrc = 3 * cells

    def gather_cells(i, carry):
        for u in range(UR):
            t = i * UR + u
            src = src_s[pl.ds(t, 1), :]
            pick = (lax.broadcasted_iota(I32, (nsrc, kpad), 0) == src).astype(F32).astype(BF16)
            r_s[t] = dot(mp, pick).astype(BF16)
        return carry

    lax.fori_loop(0, cells // UR, gather_cells, 0)

    def one_cell(t):
        cls = cls_s[pl.ds(t, 1), :]
        hot = (lax.broadcasted_iota(I32, (cpad, kpad), 0) == cls).astype(F32).astype(BF16)
        g = dot(hot, r_s[t], NT)
        for v in range(cpad // 8):
            part = g[8 * v : 8 * v + 8]
            shift, stride = (64 * (v // 8) + v % 8) * coeffs % 128, 8 * coeffs % 128
            if shift + 7 * stride >= 128:
                part = pltpu.roll(part, shift, 1)
                shift = 0
            part = pltpu.roll(part, shift, 1, stride=stride, stride_axis=0)
            g_s[pl.ds(t + 8 * v * cells, 8, stride=cells), :] = part

    def some_cells(i, carry):
        for u in range(UG):
            one_cell(i * UG + u)
        run_events("g", i, groups)
        return carry

    lax.fori_loop(0, groups, some_cells, 0)
    lane = lax.broadcasted_iota(I32, (cells, 128), 1)
    tiles = (coeffs * classes + 127) // 128
    loads[7].wait()

    def rows_of(c):
        return g_s[pl.ds(pl.multiple_of(place(c) * cells, cells), cells), :]

    def values(q):
        c = q * 128 // coeffs
        edge = (c + 1) * coeffs - q * 128
        v = jnp.where(lane < edge, rows_of(c), rows_of(jnp.minimum(c + 1, classes - 1)))
        v = jnp.where(lane < edge + coeffs, v, rows_of(jnp.minimum(c + 2, classes - 1)))
        return v.astype(BF16)

    main = (tiles - 1) // UF

    def step(i, acc):
        for u in range(0, UF, 2):
            q = i * UF + u
            o = ops_v[:, pl.ds(pl.multiple_of(q * 128, 256), 256)]
            acc = acc + dot(jnp.concatenate([values(q), values(q + 1)], axis=1), o, NT)
        run_events("f", i, main)
        return acc

    acc = lax.fori_loop(0, main, step, jnp.zeros((cells, coeffs), F32))
    for q in range(main * UF, tiles):
        end = min(q * 128 + 128, coeffs * classes)
        o = ops_v[:, q * 128 : end]
        v = values(jnp.int32(q))
        if end < q * 128 + 128:
            o = jnp.concatenate([o, jnp.zeros((coeffs, q * 128 + 128 - end), o.dtype)], axis=1)
            v = jnp.where(lane < end - q * 128, v.astype(F32), 0.0).astype(BF16)
        acc = acc + dot(v, o, NT)
    loc_o[...] = acc

    for o in [0] + order:
        for dx in dxs:
            x_wait(o, dx)
    loads[5].wait()
    loads[6].wait()

    def one_leaf(t, carry):
        tgt, px, py, pz = target_rows(*words(table, own + t, width))
        tt = jnp.transpose(tgt).astype(BF16)
        acc = jnp.zeros((width, 8), F32)
        for s in range(near):
            rows, b = source_rows(*words(table, idx_s[t, s], width))
            d = dot(tt, rows)
            r = lax.rsqrt(d)
            w = (r * r * r).astype(BF16)
            acc = acc + dot(w, b, NT)
        f = jnp.transpose(acc)
        f = f[0:4] + f[4:8]
        m = f[3:4]
        on = jnp.concatenate([act_v[pl.ds(per * t + k, 1), :] for k in range(per)], axis=1).astype(F32)
        res = jnp.concatenate([(f[0:1] - px * m), (f[1:2] - py * m), (f[2:3] - pz * m)], axis=0) * on
        acc_o[:, pl.ds(pl.multiple_of(t * width, width), width)] = res
        return carry

    lax.fori_loop(0, leaves, one_leaf, 0)
    for make, at in sent:
        make(*at).wait_send()
    for h in halo:
        h.wait_send()


UR, UG, UF = 4, 4, 8
EV_G = {1: 0, 2: 0, 3: 1, 4: 2, 5: 7}
EV_F = {6: 3, 7: 6, 8: 9}
MESH = pl.DeviceIdType.MESH
X_CHIPS = 4
REACH = 4


def on_device(positions, masses, active, near_src, multipoles, far_src, far_class, m2l_ops):
    leaves, near = near_src.shape
    particles = positions.shape[1]
    width = particles // leaves
    cells, far = far_src.shape
    coeffs = multipoles.shape[0]
    classes = m2l_ops.shape[1] // coeffs
    cpad = (classes + 63) // 64 * 64
    kpad = (far + 127) // 128 * 128
    zones, groups = lax.axis_size("zone"), lax.axis_size("grp")
    Z = groups // X_CHIPS
    cfg = (leaves, near, width, cells, far, coeffs, classes, cpad, kpad, zones, X_CHIPS, Z, REACH)
    accel, local = pl.pallas_call(
        functools.partial(kernel, cfg),
        out_shape=(jax.ShapeDtypeStruct((3, particles), F32), jax.ShapeDtypeStruct((cells, coeffs), F32)),
        in_specs=[pl.BlockSpec(memory_space=pl.ANY)] * 8,
        out_specs=(pl.BlockSpec(memory_space=pltpu.VMEM),) * 2,
        scratch_shapes=[
            pltpu.VMEM((3, particles), F32),
            pltpu.VMEM((particles // 128, 128), F32),
            pltpu.VMEM((particles // 128, 128), I32),
            pltpu.SMEM((leaves, near), I32),
            pltpu.VMEM((3, cells, coeffs), BF16),
            pltpu.VMEM((cells, far), I32),
            pltpu.VMEM((cells, far), I32),
            pltpu.VMEM(m2l_ops.shape, BF16),
            pltpu.VMEM((groups * leaves, 2, width), I32),
            pltpu.VMEM((cells, kpad), I32),
            pltpu.VMEM((cells, kpad), I32),
            pltpu.VMEM((3 * cells, 128), F32),
            pltpu.VMEM((cells, 128, kpad), BF16),
            pltpu.VMEM((cpad * cells, 128), F32),
            pltpu.SemaphoreType.DMA((8,)),
            pltpu.SemaphoreType.DMA((2,)),
            pltpu.SemaphoreType.DMA((2,)),
            pltpu.SemaphoreType.DMA((Z,)),
            pltpu.SemaphoreType.DMA((Z,)),
            pltpu.SemaphoreType.DMA(((X_CHIPS - 1) * Z,)),
            pltpu.SemaphoreType.DMA(((X_CHIPS - 1) * Z,)),
        ],
        compiler_params=pltpu.CompilerParams(
            collective_id=0, has_side_effects=True, vmem_limit_bytes=67043328),
    )(positions, masses.reshape(-1, 128), active.reshape(-1, 128), near_src, multipoles.T, far_src, far_class, m2l_ops)
    return accel, local.T


def solution(mesh):
    return jax.shard_map(
        on_device,
        mesh=mesh,
        in_specs=(
            P(None, ("zone", "grp")),
            P(("zone", "grp")),
            P(("zone", "grp")),
            P(("zone", "grp"), None),
            P(None, ("zone", "grp")),
            P(("zone", "grp"), None),
            P(("zone", "grp"), None),
            P(),
        ),
        out_specs=(P(None, ("zone", "grp")), P(None, ("zone", "grp"))),
        check_vma=False,
    )
```

time: 184 us -> 53.4 us (0.29)
  the two profiles are of different devices: /device:TPU:8 before, /device:TPU:1 now
where the time goes in v2:
time: 53.4 us; the launch traced here: 53.1 us
  Pallas kernels  49.8 us (93%)
  local copies, waits for them, and re-layouts  2.7 us (5%)
  between operations  0.64 us (1%)
    pallas_call x1, Pallas kernels, on_device(): pl.pallas_call(functools.partial(kernel, cfg), out_shape=(jax.ShapeDtypeS...  49.8 us
    unnamed x2, local copies, waits for them, and re-layouts  2.7 us

profile of v2, /device:TPU:1, one launch (start us, length us, event | category | flops | bytes accessed | tf_op | source)
XLA Modules:
  0.0 53.1 jit_solution(2970138582135186229)
XLA Ops:
  0.6 49.8 %shard_map.95 = (f32[3,2048]{1,0:T(4,128)}, f32[32,81]{1,0:T(8,128)}) custom-call(f32[3,2048]{1,0:T(4,128)} %pos_h.1, f32[16,128]{1,0:T(8,128)} %bitcast.5, s32[16,128]{1,0:T(8,128)} %bitcast.6, s32[8,8]{1,0:T(8,128)} %near_h.1, bf16[32,81]{1,0:T(8,128)(2,1)} %bitcast.7, s32[32,189]{1,0:T(8,128)} %src_h.1, s32[32,189]{1,0:T(8,128)} %cls_h.1, ...), custom_call_target="tpu_custom_call" | custom-call | tf_op jit(solution)/shard_map/pallas_call | solution.py:341
  50.4 1.4 %copy.12 = f32[3,2048]{1,0:T(4,128)} copy(f32[3,2048]{1,0:T(4,128)} %get-tuple-element.8) | data formatting | bytes 49152
  51.8 1.3 %copy.13 = f32[81,32]{0,1:T(8,128)} copy(f32[81,32]{0,1:T(8,128)} %bitcast.4) | data formatting | bytes 20736

commit v3 on v2

--- a/solution.py
+++ b/solution.py
@@ -87,7 +87,7 @@
 
 
 def kernel(cfg, pos_h, mass_h, act_h, near_h, mp_h, src_h, cls_h, ops_h, acc_o, loc_o,
-           pos_v, mass_v, act_v, idx_s, mp_v, src_v, cls_v, ops_v, table, src_s, cls_s, mp_s, r_s, g_s,
+           pos_v, mass_v, act_v, idx_s, mp_v, src_v, cls_v, ops_v, table, src_s, cls_s, mp_s, r_s, g_s, t_s, p_s, s_s, b_s, f_s,
            in_sem, halo_send, halo_recv, z_send, z_recv, x_send, x_recv):
     leaves, near, width, cells, far, coeffs, classes, cpad, kpad, zones, X, Z, R = cfg
     zone, g = lax.axis_index("zone"), lax.axis_index("grp")
@@ -154,6 +154,12 @@
             src_ref=block(o), dst_ref=block(o), send_sem=x_send.at[n], recv_sem=x_recv.at[n],
             device_id={"grp": grp_at(0, dx)}, device_id_type=MESH)
 
+    def x_onward(o, dx):
+        n = Z + o % Z
+        return pltpu.make_async_remote_copy(
+            src_ref=block(o, -dx), dst_ref=block(o, -dx), send_sem=x_send.at[n], recv_sem=x_recv.at[n],
+            device_id={"grp": grp_at(0, dx)}, device_id_type=MESH)
+
     def z_wait(o):
         n = o % Z
         pltpu.make_async_remote_copy(
@@ -166,8 +172,8 @@
             src_ref=block(o, -dx), dst_ref=block(o, -dx), send_sem=x_send.at[n], recv_sem=x_recv.at[n],
             device_id={"grp": grp_at(0, dx)}, device_id_type=MESH).wait_recv()
 
-    dxs = [d for d in (1, 3, 2) if d < X]
     sent = []
+    near_dx = (1, X - 1)
 
     def send(make, *at):
         make(*at).start()
@@ -177,35 +183,36 @@
         h.start()
     for d in reversed(reach):
         send(z_copy, 0, d)
-    for dx in dxs:
+    for dx in near_dx if 0 in RELAYS else range(1, X):
         send(x_copy, 0, dx)
+
+    def x_relay(o):
+        dx = near_dx[o % 2]
+        x_wait(o, dx)
+        send(x_onward, o, dx)
 
     def arrived(o):
         z_wait(o)
-        if o == R:
-            for d in range(plus - R, 0, -1):
-                send(z_copy, o, d)
-        if o == -R:
-            for d in range(minus - R, 0, -1):
-                send(z_copy, o, -d)
-        for dx in dxs:
+        if o % R == 0:
+            sign, most = (1, plus) if o > 0 else (-1, minus)
+            for d in range(min(R, most - abs(o)), 0, -1):
+                send(z_copy, o, sign * d)
+        for dx in near_dx[::-1]:
+            if dx == 1 and abs(o) not in RELAYS:
+                send(x_copy, o, 2)
             send(x_copy, o, dx)
 
+    order = [o for r in range(1, plus + 1) for o in (r, -r) if o <= plus and -o <= minus]
     events = {}
-    groups = cells // UG
-    order = [o for r in range(1, plus + 1) for o in (r, -r) if o <= plus and -o <= minus]
     for o in order:
-        a = abs(o)
-        where = ("g", EV_G[a]) if a in EV_G else ("f", EV_F[a])
-        events.setdefault(where, []).append(o)
-
-    def run_events(kind, i, n):
-        for k in range(n):
-            if (kind, k) in events:
-                @pl.when(i == k)
-                def _():
-                    for o in events[(kind, k)]:
-                        arrived(o)
+        events.setdefault(EVENTS.get(abs(o), "end"), []).append((arrived, o))
+    for o in [0] + order:
+        if abs(o) in RELAYS:
+            events.setdefault(RELAYS[abs(o)], []).append((x_relay, o))
+
+    def run_events(key):
+        for act, o in events.get(key, ()):
+            act(o)
 
     loads[3].wait()
     loads[4].wait()
@@ -214,6 +221,14 @@
     src_s[:, 0:far] = src_v[...]
     cls_s[:, 0:far] = place(cls_v[...])
     mp_s[...] = jnp.zeros(mp_s.shape, F32)
+
+    def target_features(t, carry):
+        tgt, px, py, pz = target_rows(*words(table, own + t, width))
+        t_s[t] = jnp.transpose(tgt).astype(BF16)
+        p_s[t] = jnp.concatenate([px, py, pz], axis=0)
+        return carry
+
+    lax.fori_loop(0, leaves, target_features, 0, unroll=True)
     for h in halo:
         h.wait_recv()
     keep = [(zone > 0).astype(F32), 1.0, (zone < zones - 1).astype(F32)]
@@ -231,6 +246,7 @@
         return carry
 
     lax.fori_loop(0, cells // UR, gather_cells, 0)
+    run_events("r")
 
     def one_cell(t):
         cls = cls_s[pl.ds(t, 1), :]
@@ -243,87 +259,93 @@
                 part = pltpu.roll(part, shift, 1)
                 shift = 0
             part = pltpu.roll(part, shift, 1, stride=stride, stride_axis=0)
-            g_s[pl.ds(t + 8 * v * cells, 8, stride=cells), :] = part
+            g_s[pl.ds(pl.multiple_of(t * cpad + 8 * v, 8), 8), :] = part
 
     def some_cells(i, carry):
         for u in range(UG):
             one_cell(i * UG + u)
-        run_events("g", i, groups)
+        for k in range(cells // UG):
+            if ("g", k) in events:
+                @pl.when(i == k)
+                def _():
+                    run_events(("g", k))
         return carry
 
-    lax.fori_loop(0, groups, some_cells, 0)
+    lax.fori_loop(0, cells // UG, some_cells, 0)
     lane = lax.broadcasted_iota(I32, (cells, 128), 1)
     tiles = (coeffs * classes + 127) // 128
     loads[7].wait()
 
     def rows_of(c):
-        return g_s[pl.ds(pl.multiple_of(place(c) * cells, cells), cells), :]
+        return g_s[pl.ds(place(c), cells, stride=cpad), :]
 
     def values(q):
         c = q * 128 // coeffs
-        edge = (c + 1) * coeffs - q * 128
-        v = jnp.where(lane < edge, rows_of(c), rows_of(jnp.minimum(c + 1, classes - 1)))
-        v = jnp.where(lane < edge + coeffs, v, rows_of(jnp.minimum(c + 2, classes - 1)))
+        v = rows_of(c)
+        while (c + 1) * coeffs < min(q * 128 + 128, coeffs * classes):
+            c += 1
+            v = jnp.where(lane < c * coeffs - q * 128, v, rows_of(c))
+        if (c + 1) * coeffs < q * 128 + 128:
+            v = jnp.where(lane < (c + 1) * coeffs - q * 128, v, 0.0)
         return v.astype(BF16)
 
-    main = (tiles - 1) // UF
-
-    def step(i, acc):
-        for u in range(0, UF, 2):
-            q = i * UF + u
-            o = ops_v[:, pl.ds(pl.multiple_of(q * 128, 256), 256)]
-            acc = acc + dot(jnp.concatenate([values(q), values(q + 1)], axis=1), o, NT)
-        run_events("f", i, main)
-        return acc
-
-    acc = lax.fori_loop(0, main, step, jnp.zeros((cells, coeffs), F32))
-    for q in range(main * UF, tiles):
-        end = min(q * 128 + 128, coeffs * classes)
+    acc = jnp.zeros((cells, coeffs), F32)
+    for q in range(0, tiles, 2):
+        run_events(("f", q // 2))
+        end = min(q * 128 + 256, coeffs * classes)
         o = ops_v[:, q * 128 : end]
-        v = values(jnp.int32(q))
-        if end < q * 128 + 128:
-            o = jnp.concatenate([o, jnp.zeros((coeffs, q * 128 + 128 - end), o.dtype)], axis=1)
-            v = jnp.where(lane < end - q * 128, v.astype(F32), 0.0).astype(BF16)
-        acc = acc + dot(v, o, NT)
+        if end < q * 128 + 256:
+            o = jnp.concatenate([o[:, :128], o[:, 128:], jnp.zeros((coeffs, q * 128 + 256 - end), o.dtype)], axis=1)
+        acc = acc + dot(jnp.concatenate([values(q), values(q + 1)], axis=1), o, NT)
     loc_o[...] = acc
-
-    for o in [0] + order:
-        for dx in dxs:
-            x_wait(o, dx)
+    run_events("end")
+
     loads[5].wait()
     loads[6].wait()
-
-    def one_leaf(t, carry):
-        tgt, px, py, pz = target_rows(*words(table, own + t, width))
-        tt = jnp.transpose(tgt).astype(BF16)
-        acc = jnp.zeros((width, 8), F32)
-        for s in range(near):
-            rows, b = source_rows(*words(table, idx_s[t, s], width))
-            d = dot(tt, rows)
-            r = lax.rsqrt(d)
-            w = (r * r * r).astype(BF16)
-            acc = acc + dot(w, b, NT)
-        f = jnp.transpose(acc)
+    for o in [0] + order:
+        for dx in range(1, X):
+            if not (abs(o) in RELAYS and dx == near_dx[o % 2]):
+                x_wait(o, dx)
+
+    def source_features(i, carry):
+        for u in range(US):
+            n = i * US + u
+            rows, b = source_rows(*words(table, idx_s[n // near, n % near], width))
+            s_s[n] = rows
+            b_s[n] = b
+        return carry
+
+    lax.fori_loop(0, leaves * near // US, source_features, 0)
+
+    def some_leaves(i, carry):
+        for u in range(UL):
+            t = i * UL + u
+            acc = jnp.zeros((width, 8), F32)
+            for s in range(near):
+                n = t * near + s
+                r = lax.rsqrt(dot(t_s[t], s_s[n]))
+                acc = acc + dot((r * r * r).astype(BF16), b_s[n], NT)
+            f_s[t] = acc
+        return carry
+
+    lax.fori_loop(0, leaves // UL, some_leaves, 0)
+    for t in range(leaves):
+        f = jnp.transpose(f_s[t])
         f = f[0:4] + f[4:8]
-        m = f[3:4]
-        on = jnp.concatenate([act_v[pl.ds(per * t + k, 1), :] for k in range(per)], axis=1).astype(F32)
-        res = jnp.concatenate([(f[0:1] - px * m), (f[1:2] - py * m), (f[2:3] - pz * m)], axis=0) * on
-        acc_o[:, pl.ds(pl.multiple_of(t * width, width), width)] = res
-        return carry
-
-    lax.fori_loop(0, leaves, one_leaf, 0)
+        on = jnp.concatenate([act_v[per * t + k : per * t + k + 1, :] for k in range(per)], axis=1).astype(F32)
+        acc_o[:, t * width : (t + 1) * width] = (f[0:3] - p_s[t] * f[3:4]) * on
     for make, at in sent:
         make(*at).wait_send()
     for h in halo:
         h.wait_send()
 
 
-UR, UG, UF = 4, 4, 8
-EV_G = {1: 0, 2: 0, 3: 1, 4: 2, 5: 7}
-EV_F = {6: 3, 7: 6, 8: 9}
+UR, UG, US, UL = 16, 8, 8, 4
+EVENTS = {1: ("g", 0), 2: ("g", 0), 3: ("g", 0), 4: ("f", 45), 5: ("f", 45), 6: ("f", 45)}
+RELAYS = {}
 MESH = pl.DeviceIdType.MESH
 X_CHIPS = 4
-REACH = 4
+REACH = 3
 
 
 def on_device(positions, masses, active, near_src, multipoles, far_src, far_class, m2l_ops):
@@ -358,6 +380,11 @@
             pltpu.VMEM((3 * cells, 128), F32),
             pltpu.VMEM((cells, 128, kpad), BF16),
             pltpu.VMEM((cpad * cells, 128), F32),
+            pltpu.VMEM((leaves, width, 32), BF16),
+            pltpu.VMEM((leaves, 3, width), F32),
+            pltpu.VMEM((leaves * near, 32, width), BF16),
+            pltpu.VMEM((leaves * near, 8, width), BF16),
+            pltpu.VMEM((leaves, width, 8), F32),
             pltpu.SemaphoreType.DMA((8,)),
             pltpu.SemaphoreType.DMA((2,)),
             pltpu.SemaphoreType.DMA((2,)),
@@ -369,7 +396,29 @@
         compiler_params=pltpu.CompilerParams(
             collective_id=0, has_side_effects=True, vmem_limit_bytes=67043328),
     )(positions, masses.reshape(-1, 128), active.reshape(-1, 128), near_src, multipoles.T, far_src, far_class, m2l_ops)
+    accel, local = pl.pallas_call(
+        hand_over,
+        out_shape=(jax.ShapeDtypeStruct(accel.shape, F32), jax.ShapeDtypeStruct(local.shape, F32)),
+        in_specs=[pl.BlockSpec(memory_space=pl.ANY)] * 2,
+        out_specs=(pl.BlockSpec(memory_space=pl.ANY),) * 2,
+        scratch_shapes=[pltpu.VMEM(accel.shape, F32), pltpu.VMEM(local.shape, F32), pltpu.SemaphoreType.DMA((4,))],
+    )(accel, local)
     return accel, local.T
+
+
+def hand_over(a_in, b_in, a_out, b_out, a_v, b_v, sem):
+    copies = [
+        pltpu.make_async_copy(x, y, sem.at[n])
+        for n, (x, y) in enumerate([(a_in, a_v), (b_in, b_v), (a_v, a_out), (b_v, b_out)])
+    ]
+    copies[0].start()
+    copies[1].start()
+    copies[1].wait()
+    copies[3].start()
+    copies[0].wait()
+    copies[2].start()
+    copies[2].wait()
+    copies[3].wait()
 
 
 def solution(mesh):

time: 53.4 us -> 46.9 us (0.88)
  Pallas kernels: 49.8 us -> 45.8 us
  local copies, waits for them, and re-layouts: 2.7 us -> 0 us
    pallas_call x1, Pallas kernels: 49.8 us -> 44.4 us  [on_device(): pl.pallas_call(functools.partial(kernel, cfg), out_shape=(jax.ShapeDtypeS...]
    unnamed x2 -> x0, local copies, waits for them, and re-layouts: 2.7 us -> none
    pallas_call x0 -> x1, Pallas kernels: none -> 1.41 us  [on_device(): pl.pallas_call(hand_over, out_shape=(jax.ShapeDtypeStruct(accel.shape, F3...]
where the time goes in v3:
time: 46.9 us; the launch traced here: 46.4 us
  Pallas kernels  45.8 us (98%)
  between operations  0.64 us (1%)
    pallas_call x1, Pallas kernels, on_device(): pl.pallas_call(functools.partial(kernel, cfg), out_shape=(jax.ShapeDtypeS...  44.4 us
    pallas_call x1, Pallas kernels, on_device(): pl.pallas_call(hand_over, out_shape=(jax.ShapeDtypeStruct(accel.shape, F3...  1.41 us

profile of v3, /device:TPU:1, one launch (start us, length us, event | category | flops | bytes accessed | tf_op | source)
XLA Modules:
  0.0 46.4 jit_solution(15588951012885437754)
XLA Ops:
  0.6 44.4 %shard_map.95 = (f32[3,2048]{1,0:T(4,128)}, f32[32,81]{1,0:T(8,128)}) custom-call(f32[3,2048]{1,0:T(4,128)} %pos_h.1, f32[16,128]{1,0:T(8,128)} %bitcast.4, s32[16,128]{1,0:T(8,128)} %bitcast.5, s32[8,8]{1,0:T(8,128)} %near_h.1, bf16[32,81]{1,0:T(8,128)(2,1)} %bitcast.6, s32[32,189]{1,0:T(8,128)} %src_h.1, s32[32,189]{1,0:T(8,128)} %cls_h.1, ...), custom_call_target="tpu_custom_call" | custom-call | tf_op jit(solution)/shard_map/pallas_call | solution.py:363
  45.0 1.4 %shard_map.96 = (f32[3,2048]{1,0:T(4,128)}, f32[32,81]{1,0:T(8,128)}) custom-call(f32[3,2048]{1,0:T(4,128)} %get-tuple-element.6.a_in, f32[32,81]{1,0:T(8,128)} %get-tuple-element.7.b_in), custom_call_target="tpu_custom_call" | custom-call | tf_op jit(solution)/shard_map/pallas_call | solution.py:399

commit v4 on v3

--- a/solution.py
+++ b/solution.py
@@ -204,7 +204,7 @@
 
     order = [o for r in range(1, plus + 1) for o in (r, -r) if o <= plus and -o <= minus]
     events = {}
-    for o in order:
+    for o in sorted(order, key=lambda o: o % R != 0):
         events.setdefault(EVENTS.get(abs(o), "end"), []).append((arrived, o))
     for o in [0] + order:
         if abs(o) in RELAYS:

time: 46.9 us -> 47.1 us (level)
  no operation moved by 1% of the time
where the time goes in v4:
time: 47.1 us; the launch traced here: 46.4 us
  Pallas kernels  45.8 us (97%)
  between operations  0.64 us (1%)
    pallas_call x1, Pallas kernels, on_device(): pl.pallas_call(functools.partial(kernel, cfg), out_shape=(jax.ShapeDtypeS...  44.4 us
    pallas_call x1, Pallas kernels, on_device(): pl.pallas_call(hand_over, out_shape=(jax.ShapeDtypeStruct(accel.shape, F3...  1.41 us

profile of v4, /device:TPU:1, one launch (start us, length us, event | category | flops | bytes accessed | tf_op | source)
XLA Modules:
  0.0 46.4 jit_solution(327761903984851822)
XLA Ops:
  0.6 44.4 %shard_map.95 = (f32[3,2048]{1,0:T(4,128)}, f32[32,81]{1,0:T(8,128)}) custom-call(f32[3,2048]{1,0:T(4,128)} %pos_h.1, f32[16,128]{1,0:T(8,128)} %bitcast.4, s32[16,128]{1,0:T(8,128)} %bitcast.5, s32[8,8]{1,0:T(8,128)} %near_h.1, bf16[32,81]{1,0:T(8,128)(2,1)} %bitcast.6, s32[32,189]{1,0:T(8,128)} %src_h.1, s32[32,189]{1,0:T(8,128)} %cls_h.1, ...), custom_call_target="tpu_custom_call" | custom-call | tf_op jit(solution)/shard_map/pallas_call | solution.py:363
  45.0 1.4 %shard_map.96 = (f32[3,2048]{1,0:T(4,128)}, f32[32,81]{1,0:T(8,128)}) custom-call(f32[3,2048]{1,0:T(4,128)} %get-tuple-element.6.a_in, f32[32,81]{1,0:T(8,128)} %get-tuple-element.7.b_in), custom_call_target="tpu_custom_call" | custom-call | tf_op jit(solution)/shard_map/pallas_call | solution.py:399
